TPU v7x, 32 devices: a whole 2x2x4 slice. The times are simulated.
32 devices in a mesh: seq: 8 (over z, x), wsh: 4 (over y, core).
Axes of the slice: x: 2, y: 2, z: 4, core: 2. Of those that a mesh axis runs over, the one named last changes fastest.
Arguments:
- tokens_in: bfloat16 [4, 4096, 1024], P('wsh', 'seq'), may hold values from -6 to 6
- out_grad: bfloat16 [4, 4096, 1024], P('wsh', 'seq'), may hold values from -6 to 6
- deal_order: int32 [8], replicated, may hold values from 0 to 7, each once
- seq_lengths: int32 [4, 4], P('wsh'), may hold values from 1 to 2048, 4096 in all within a row
- weights: bfloat16 [1024, 17920], P('wsh'), may hold values from -0.1875 to 0.1875
- norm_gains: bfloat16 [2, 1024], P(None, 'wsh'), may hold values from 0.5 to 1.5
- conv_kernel: bfloat16 [3, 1024], P(None, 'wsh'), may hold values from -3 to 3
- vector_state: float32 [5, 1024], P(None, 'wsh'), may hold values from 0.2 to 5
- kron_stats: float32 [2, 1120, 128, 128], P(None, 'wsh', 'seq'), may hold values from -6 to 6
- kron_roots: float32 [2, 1120, 128, 128], P(None, 'wsh', 'seq'), as said below
Outputs:
- block_out: bfloat16 [4, 4096, 1024], P('wsh', 'seq')
- input_grad: bfloat16 [4, 4096, 1024], P('wsh', 'seq')
- weight_grad: float32 [1024, 17920], P('wsh')
- vector_grad: float32 [5, 1024], P(None, 'wsh')
- vector_state_new: float32 [5, 1024], P(None, 'wsh')
- vector_update: float32 [5, 1024], P(None, 'wsh')
- kron_stats_new: float32 [2, 1120, 128, 128], P(None, 'wsh', 'seq')
- weight_update: float32 [1120, 128, 128], P('wsh', 'seq')
Inputs may be any that keep to these rules, and one draw needn't show every extreme that they name: `deal_order`: a permutation of 0 to 7. `seq_lengths`: each row sums to 4096; in every pack the longest sequence has exactly 2048 tokens. `kron_roots`: each block has a dominant diagonal between 0.5 and 2.
All inputs are finite; a program needn't handle non-finite values.
Results may differ from a plain program's by a relative error of at most 0.025.
Values may be sent and summed in bfloat16 or wider, within the bound.
A program may use at most 320 MiB of HBM per device.

v0:
```python
import jax
import jax.numpy as jnp
from jax import lax
from jax.sharding import PartitionSpec as P

D = 1024
FF = 4608
BLK = 128
EPS = 1e-05
BETA = 0.5
BETA_VEC = 0.5
LEARN = 0.03
LEARN_VEC = 0.05
HIGH = lax.Precision.HIGHEST


def passed_along(block, axis, distance):
    devices = range(lax.axis_size(axis))
    route = [(i - distance, i) for i in devices if i - distance in devices]
    return lax.ppermute(block, axis, route)


def seq_positions(lengths_row, first, count):
    starts = jnp.cumsum(lengths_row) - lengths_row
    rows_at = first + jnp.arange(count, dtype=jnp.int32)
    begin = jnp.max(jnp.where(starts[None, :] <= rows_at[:, None], starts[None, :], 0), axis=1)
    return rows_at - begin


def rms_scale(values):
    return lax.rsqrt(jnp.mean(values * values, axis=1, keepdims=True) + EPS)


def norm_back(upstream, values, scale, gain):
    scaled = upstream * gain
    inner = jnp.mean(scaled * values, axis=1, keepdims=True)
    return (
        scale * scaled - values * scale * scale * scale * inner,
        jnp.sum(upstream * values * scale, axis=0),
    )


def contract_rows(left, right):
    return lax.dot_general(
        left, right, (((0,), (0,)), ((), ())), preferred_element_type=jnp.float32
    )


def contract_cols(left, right):
    return lax.dot_general(
        left, right, (((1,), (1,)), ((), ())), preferred_element_type=jnp.float32
    )


def shards(
    tokens_in,
    out_grad,
    deal_order,
    seq_lengths,
    weights,
    norm_gains,
    conv_kernel,
    vector_state,
    kron_stats,
    kron_roots,
):
    n_seq = lax.axis_size("seq")
    n_wsh = lax.axis_size("wsh")
    rows = tokens_in.shape[1]
    unit = rows // n_seq
    arrived = (
        lax.all_to_all(
            tokens_in.reshape(n_seq, unit, D), "seq", split_axis=0, concat_axis=0, tiled=True
        ),
        lax.all_to_all(
            out_grad.reshape(n_seq, unit, D), "seq", split_axis=0, concat_axis=0, tiled=True
        ),
    )
    x_bf = jnp.take(arrived[0], deal_order, axis=0).reshape(rows, D)
    dy_bf = jnp.take(arrived[1], deal_order, axis=0).reshape(rows, D)
    full_w, gains_bf, kernel_bf = (
        lax.all_gather(weights, "wsh", axis=0, tiled=True),
        lax.all_gather(norm_gains, "wsh", axis=1, tiled=True),
        lax.all_gather(conv_kernel, "wsh", axis=1, tiled=True),
    )
    gains = gains_bf.astype(jnp.float32)
    kernel = kernel_bf.astype(jnp.float32)
    first_row = lax.axis_index("seq") * rows
    pos = seq_positions(seq_lengths[0], first_row, rows + 2)
    masks = [(pos >= 2 - k).astype(jnp.float32)[:, None] for k in range(3)]
    xf = x_bf.astype(jnp.float32)
    scale_one = rms_scale(xf)
    xn = (xf * scale_one * gains[0]).astype(jnp.bfloat16)
    proj = jnp.dot(xn, full_w[:, : 3 * D], preferred_element_type=jnp.float32)
    b_part = proj[:, :D]
    c_part = proj[:, D : 2 * D]
    x_part = proj[:, 2 * D :]
    conv_in = b_part * x_part
    prev = passed_along(conv_in[rows - 2 :], "seq", 1)
    ext = jnp.concatenate([prev, conv_in], axis=0)
    conv = (
        kernel[0] * masks[0][:rows] * ext[0:rows]
        + kernel[1] * masks[1][:rows] * ext[1 : rows + 1]
        + kernel[2] * masks[2][:rows] * ext[2 : rows + 2]
    )
    yc = (c_part * conv).astype(jnp.bfloat16)
    hidden_sum = xf + jnp.dot(yc, full_w[:, 3 * D : 4 * D], preferred_element_type=jnp.float32)
    scale_two = rms_scale(hidden_sum)
    hn = (hidden_sum * scale_two * gains[1]).astype(jnp.bfloat16)
    gate_up = jnp.dot(hn, full_w[:, 4 * D : 4 * D + 2 * FF], preferred_element_type=jnp.float32)
    gate = gate_up[:, :FF]
    upper = gate_up[:, FF:]
    sig = jax.nn.sigmoid(gate)
    act = (gate * sig * upper).astype(jnp.bfloat16)
    ffn = contract_cols(act, full_w[:, 4 * D + 2 * FF :])
    result = (hidden_sum + ffn).astype(jnp.bfloat16)
    g_down = contract_rows(dy_bf, act)
    d_act = jnp.dot(dy_bf, full_w[:, 4 * D + 2 * FF :], preferred_element_type=jnp.float32)
    d_gate = d_act * upper * sig * (1.0 + gate * (1.0 - sig))
    d_upper = d_act * gate * sig
    d_gu = jnp.concatenate([d_gate, d_upper], axis=1).astype(jnp.bfloat16)
    g_gu = contract_rows(hn, d_gu)
    d_hn = contract_cols(d_gu, full_w[:, 4 * D : 4 * D + 2 * FF])
    d_norm_two, g_gain_two = norm_back(d_hn, hidden_sum, scale_two, gains[1])
    d_hidden = dy_bf.astype(jnp.float32) + d_norm_two
    d_mix = d_hidden.astype(jnp.bfloat16)
    g_out = contract_rows(yc, d_mix)
    d_yc = contract_cols(d_mix, full_w[:, 3 * D : 4 * D])
    d_c = d_yc * conv
    d_conv = d_yc * c_part
    after = passed_along(d_conv[:2], "seq", -1)
    d_ext = jnp.concatenate([d_conv, after], axis=0)
    weighted = [d_ext * masks[k] for k in range(3)]
    d_bx = (
        kernel[2] * weighted[2][:rows]
        + kernel[1] * weighted[1][1 : rows + 1]
        + kernel[0] * weighted[0][2 : rows + 2]
    )
    g_taps = jnp.stack([jnp.sum(weighted[k][:rows] * ext[k : k + rows], axis=0) for k in range(3)])
    d_proj = jnp.concatenate([d_bx * x_part, d_c, d_bx * b_part], axis=1).astype(jnp.bfloat16)
    g_in = contract_rows(xn, d_proj)
    d_xn = contract_cols(d_proj, full_w[:, : 3 * D])
    d_norm_one, g_gain_one = norm_back(d_xn, xf, scale_one, gains[0])
    d_input = (d_hidden + d_norm_one).astype(jnp.bfloat16)
    g_vec = jnp.concatenate([g_gain_one[None], g_gain_two[None], g_taps], axis=0)
    inverse = jnp.argsort(deal_order)
    leaving = (
        jnp.take(result.reshape(n_seq, unit, D), inverse, axis=0),
        jnp.take(d_input.reshape(n_seq, unit, D), inverse, axis=0),
    )
    returned = (
        lax.all_to_all(leaving[0], "seq", split_axis=0, concat_axis=0, tiled=True),
        lax.all_to_all(leaving[1], "seq", split_axis=0, concat_axis=0, tiled=True),
    )
    summed = (
        lax.psum_scatter(g_in.astype(jnp.bfloat16), "wsh", scatter_dimension=0, tiled=True).astype(
            jnp.float32
        ),
        lax.psum_scatter(g_out.astype(jnp.bfloat16), "wsh", scatter_dimension=0, tiled=True).astype(
            jnp.float32
        ),
        lax.psum_scatter(g_gu.astype(jnp.bfloat16), "wsh", scatter_dimension=0, tiled=True).astype(
            jnp.float32
        ),
        lax.psum_scatter(
            g_down.astype(jnp.bfloat16), "wsh", scatter_dimension=0, tiled=True
        ).astype(jnp.float32),
        lax.psum_scatter(g_vec.astype(jnp.bfloat16), "wsh", scatter_dimension=1, tiled=True).astype(
            jnp.float32
        ),
    )
    summed = (
        lax.psum(summed[0].astype(jnp.bfloat16), "seq").astype(jnp.float32),
        lax.psum(summed[1].astype(jnp.bfloat16), "seq").astype(jnp.float32),
        lax.psum(summed[2].astype(jnp.bfloat16), "seq").astype(jnp.float32),
        lax.psum(summed[3].astype(jnp.bfloat16), "seq").astype(jnp.float32),
        lax.psum(summed[4].astype(jnp.bfloat16), "seq").astype(jnp.float32),
    )
    grad_scale = lax.rsqrt(jnp.asarray(rows * n_seq * n_wsh, jnp.float32))
    grad_shard = jnp.concatenate([summed[0], summed[1], summed[2], summed[3]], axis=1) * grad_scale
    vec_grad = summed[4] * grad_scale
    state_new = BETA_VEC * vector_state + (1.0 - BETA_VEC) * vec_grad * vec_grad
    vec_update = -LEARN_VEC * vec_grad * lax.rsqrt(state_new)
    nrow_blocks = grad_shard.shape[0] // BLK
    ncol_blocks = grad_shard.shape[1] // BLK
    grad_blocks = (
        grad_shard.reshape(nrow_blocks, BLK, ncol_blocks, BLK)
        .transpose(0, 2, 1, 3)
        .reshape(nrow_blocks * ncol_blocks, BLK, BLK)
    )
    share = BLK // n_seq
    first_block_row = lax.axis_index("seq") * share
    block_rows = lax.dynamic_slice_in_dim(grad_blocks, first_block_row, share, 1)
    block_cols = lax.dynamic_slice_in_dim(grad_blocks, first_block_row, share, 2)
    left_term = jnp.einsum("nij,nkj->nik", block_rows, grad_blocks, precision=HIGH)
    right_term = jnp.einsum("nji,njk->nik", block_cols, grad_blocks, precision=HIGH)
    stats_new = jnp.stack(
        [
            BETA * kron_stats[0] + (1.0 - BETA) * left_term / BLK,
            BETA * kron_stats[1] + (1.0 - BETA) * right_term / BLK,
        ]
    )
    right_full = lax.all_gather(
        kron_roots[1].astype(jnp.bfloat16), "seq", axis=1, tiled=True
    ).astype(jnp.float32)
    left_mul = jnp.einsum("nij,njk->nik", kron_roots[0], grad_blocks, precision=HIGH)
    update = -LEARN * jnp.einsum("nij,njk->nik", left_mul, right_full, precision=HIGH)
    return (
        returned[0].reshape(1, rows, D),
        returned[1].reshape(1, rows, D),
        grad_shard,
        vec_grad,
        state_new,
        vec_update,
        stats_new,
        update,
    )


def solution(mesh):
    return jax.shard_map(
        shards,
        mesh=mesh,
        in_specs=(
            P("wsh", "seq", None),
            P("wsh", "seq", None),
            P(),
            P("wsh", None),
            P("wsh", None),
            P(None, "wsh"),
            P(None, "wsh"),
            P(None, "wsh"),
            P(None, "wsh", "seq", None),
            P(None, "wsh", "seq", None),
        ),
        out_specs=(
            P("wsh", "seq", None),
            P("wsh", "seq", None),
            P("wsh", None),
            P(None, "wsh"),
            P(None, "wsh"),
            P(None, "wsh"),
            P(None, "wsh", "seq", None),
            P("wsh", "seq", None),
        ),
        check_vma=False,
    )
```

profile of v0, /device:TPU:0, one launch (start us, length us, event | category | flops | bytes accessed | tf_op | source)
XLA Modules:
  0.0 1136.9 jit_solution(3107054169689322003)
XLA Ops:
  7.2 0.7 all-gather.4.cloned.1.call-update
  7.9 7.4 all-to-all-start
  15.6 25.6 %all-to-all-done = bf16[8,64,1024]{2,1,0:T(8,128)(2,1)S(1)} async-done(((bf16[8,64,1024]{2,1,0:T(8,128)(2,1)}), bf16[8,64,1024]{2,1,0:T(8,128)(2,1)S(1)}, u32[]{:S(2)}, u32[]{:S(2)}) %all-to-all-start) | async-done | bytes 1048608 | tf_op jit(solution)/shard_map/all_to_all | solution.py:72
  41.1 4.3 all-to-all-start.2
  45.6 5.2 all_gather.12
  50.8 5.3 all_gather.14
  56.2 0.6 gather_fusion
  57.4 13.6 %all-to-all-done.2 = bf16[8,64,1024]{2,1,0:T(8,128)(2,1)} async-done(((bf16[8,64,1024]{2,1,0:T(8,128)(2,1)}), bf16[8,64,1024]{2,1,0:T(8,128)(2,1)}, u32[]{:S(2)}, u32[]{:S(2)}) %all-to-all-start.2) | async-done | bytes 1048608 | tf_op jit(solution)/shard_map/all_to_all | solution.py:75
  71.0 2.8 gather_fusion.2
  74.1 159.7 %all-gather.4.cloned.1.call-done = bf16[1024,17920]{1,0:T(8,128)(2,1)} async-done(((bf16[256,17920]{1,0:T(8,128)(2,1)}), bf16[1024,17920]{1,0:T(8,128)(2,1)}) %all-gather.4.cloned.1.call-update) | async-done | bytes 36700176 | tf_op jit(solution)/shard_map/all_gather | solution.py:82
  233.8 5.5 fusion.14
  239.3 0.5 slice_multiply_fusion.4
  239.8 3.7 collective-permute-start
  243.5 1.1 broadcast_select_fusion.2
  244.7 2.3 multiply_convert_fusion.7
  247.0 3.3 multiply_reduce_fusion.3
  250.3 18.3 %fusion.4 = f32[512,9216]{1,0:T(8,128)} fusion(bf16[1024,17920]{1,0:T(8,128)(2,1)} %all-gather.4.cloned.1.call-done, f32[512,1024]{1,0:T(8,128)S(1)} %get-tuple-element.51, f32[1024]{0:T(1024)S(1)} %bitcast.99, f32[512]{0:T(512)S(1)} %add_rsqrt_fusion.1), kind=kOutput, calls=%fused_computation.10 | convolution fusion | flops 9665249280 | bytes 39852032 | tf_op jit(solution)/shard_map/dot_general | solution.py:110
  268.6 17.8 %multiply_convert_fusion.1 = (bf16[512,4608]{1,0:T(8,128)(2,1)}, bf16[512,4608]{1,0:T(8,128)(2,1)}, bf16[512,4608]{1,0:T(8,128)(2,1)}) fusion(f32[512,9216]{1,0:T(8,128)} %fusion.4, bf16[512,1024]{1,0:T(8,128)(2,1)} %bitcast.86, bf16[1024,17920]{1,0:T(8,128)(2,1)} %all-gather.4.cloned.1.call-done), kind=kOutput, calls=%fused_computation.15 | convolution fusion | flops 4869586944 | bytes 43515904 | tf_op jit(solution)/shard_map/dot_general | solution.py:118
  286.4 16.0 %multiply_reduce_fusion.1 = (bf16[1024]{0:T(1024)(128)(2,1)S(1)}, f32[512]{0:T(512)S(1)}, f32[512,1024]{1,0:T(8,128)S(1)}) fusion(f32[512,1024]{1,0:T(8,128)} %copy-done.10, f32[512]{0:T(512)S(1)} %add_rsqrt_fusion.1, f32[1024]{0:T(1024)S(1)} %bitcast.100, bf16[1024,17920]{1,0:T(8,128)(2,1)} %all-gather.4.cloned.1.call-done, ...), kind=kOutput, calls=%fused_computation.75 | convolution fusion | flops 9685694464 | bytes 32516096 | tf_op jit(solution)/shard_map/dot_general | solution.py:50
  302.4 0.7 subtract_add_fusion
  303.2 1.5 copy-done.2
  304.7 2.6 convolution_convert_fusion.3
  307.4 3.7 fusion.42
  311.1 2.4 multiply_convert_fusion.4
  313.5 1.3 collective-permute-start.1
  314.8 4.5 collective-permute-done.1
  319.7 2.6 fusion.26
  322.3 0.5 multiply_convert_fusion.3
  323.3 0.5 copy-done.15
  324.2 5.7 convolution_convert_fusion.2
  330.0 1.1 copy-done.9
  331.1 9.8 convolution_convert_fusion.1
  341.0 1.5 copy-done.12
  342.6 17.8 %convolution_convert_fusion = bf16[1024,9216]{1,0:T(8,128)(2,1)} fusion(bf16[512,4608]{1,0:T(8,128)(2,1)} %get-tuple-element.32, bf16[512,4608]{1,0:T(8,128)(2,1)} %get-tuple-element.31, f32[512,1024]{1,0:T(8,128)S(1)} %copy-done.12, f32[1024]{0:T(1024)S(1)} %bitcast.102, f32[512]{0:T(512)S(1)} %add_rsqrt_fusion.1), kind=kOutput, calls=%fused_computation.7 | convolution fusion | flops 9693560832 | bytes 30414848 | tf_op jit(solution)/shard_map/dot_general | solution.py:44
  360.4 9.6 fusion.41
  370.1 0.6 concatenate.30
  370.8 30.0 %reduce-scatter.6.cloned.1.call-done = bf16[256,3072]{1,0:T(8,128)(2,1)} async-done(((bf16[1024,3072]{1,0:T(8,128)(2,1)}), bf16[256,3072]{1,0:T(8,128)(2,1)}) %reduce-scatter.6.cloned.1.call-update) | async-done | bytes 1572880 | tf_op jit(solution)/shard_map/reduce_scatter | solution.py:156
  400.9 81.0 %reduce-scatter.12.cloned.1.call-done = bf16[256,4608]{1,0:T(8,128)(2,1)} async-done(((bf16[1024,4608]{1,0:T(8,128)(2,1)}), bf16[256,4608]{1,0:T(8,128)(2,1)}) %reduce-scatter.12.cloned.1.call-update) | async-done | bytes 2359312 | tf_op jit(solution)/shard_map/reduce_scatter | solution.py:165
  481.9 140.3 %reduce-scatter.10.cloned.1.call-done = bf16[256,9216]{1,0:T(8,128)(2,1)} async-done(((bf16[1024,9216]{1,0:T(8,128)(2,1)}), bf16[256,9216]{1,0:T(8,128)(2,1)}) %reduce-scatter.10.cloned.1.call-update) | async-done | bytes 4718608 | tf_op jit(solution)/shard_map/reduce_scatter | solution.py:162
  622.3 2.8 slice.250
  625.1 1.0 sort.17
  626.1 9.9 add_convert_fusion
  636.0 3.0 gather_fusion.1
  638.9 3.3 fusion.37
  642.2 1.9 gather_fusion.3
  644.1 1.2 broadcast_select_fusion
  645.4 58.2 %all_to_all.20 = bf16[8,64,1024]{2,1,0:T(8,128)(2,1)S(1)} all-to-all(bf16[8,64,1024]{2,1,0:T(8,128)(2,1)S(1)} %get-tuple-element.49), channel_id=1, replica_groups=mesh['seq'=8,'wsh'=4] {'seq'}, dimensions={0} | all-to-all | bytes 2097152 | tf_op jit(solution)/shard_map/all_to_all | solution.py:152
  703.6 3.7 all-to-all-start.3
  707.3 49.4 %psum.39 = bf16[5,256]{1,0:T(8,128)(2,1)S(1)} all-reduce(bf16[5,256]{1,0:T(8,128)(2,1)} %reduce-scatter.14.cloned.1.call-done), channel_id=1, replica_groups=mesh['seq'=8,'wsh'=4] {'seq'}, use_global_device_ids=true, to_apply=%region_21.23 | all-reduce | flops 1280 | bytes 5120 | tf_op jit(solution)/shard_map/psum | solution.py:177
  756.7 0.6 fusion.63
  757.3 0.9 all-to-all-done.3
  758.3 222.7 %all-reduce.3.cloned.1.call-done = (bf16[256,4608]{1,0:T(8,128)(2,1)}, bf16[256,9216]{1,0:T(8,128)(2,1)}, bf16[256,1024]{1,0:T(8,128)(2,1)}, bf16[256,3072]{1,0:T(8,128)(2,1)}) async-done(((bf16[256,4608]{1,0:T(8,128)(2,1)}, bf16[256,9216]{1,0:T(8,128)(2,1)}, bf16[256,1024]{1,0:T(8,128)(2,1)}, bf16[256,3072]{1,0:T(8,128)(2,1)}), (bf16[256,4608]{1,0:T(8,128)(2,1)}, bf16[256,9216]{1,0:T(8,128)(2,1)}, ...) | async-done | bytes 9175056 | tf_op jit(solution)/shard_map/psum | solution.py:176
  980.9 10.2 convert_multiply_fusion
  991.1 19.2 %mul.433 = f32[2,128,140,128]{3,2,1,0:T(8,128)} reshape(f32[256,17920]{1,0:T(8,128)} %convert_multiply_fusion) | data formatting | bytes 36700160 | tf_op jit(solution)/shard_map/mul | solution.py:180
  1010.3 12.0 %copy.22 = f32[2,140,128,128]{3,2,1,0:T(8,128)S(1)} copy(f32[2,140,128,128]{3,1,2,0:T(8,128)} %bitcast.79) | data formatting | bytes 36700160 | tf_op jit(solution)/shard_map/transpose | solution.py:188
  1022.4 29.2 %fusion.19 = f32[1,280,16,128]{3,2,1,0:T(8,128)S(1)} fusion(f32[2,280,16,128]{3,2,1,0:T(8,128)S(1)} %bitcast.83, f32[280,128,128]{2,1,0:T(8,128)S(1)} %bitcast.76, s32[]{:T(128)S(6)} %select_n.16), kind=kOutput, calls=%fused_computation.39 | convolution fusion | flops 882524160 | bytes 25231364 | tf_op jit(solution)/shard_map/nij,nkj->nik/dot_general | solution.py:195
  1051.6 35.4 %fusion.18 = f32[1,280,16,128]{3,2,1,0:T(8,128)S(1)} fusion(f32[2,280,16,128]{3,2,1,0:T(8,128)S(1)} %bitcast.83, f32[280,128,128]{2,1,0:T(8,128)S(1)} %bitcast.77, s32[]{:T(128)S(6)} %select_n.16), kind=kOutput, calls=%fused_computation.37 | convolution fusion | flops 882524160 | bytes 41287684 | tf_op jit(solution)/shard_map/nji,njk->nik/dot_general | solution.py:196
  1087.0 2.4 pad_maximum_fusion.3
  1089.5 17.0 %fusion.16 = f32[280,128,16]{1,2,0:T(8,128)S(1)} fusion(f32[280,128,128]{2,1,0:T(8,128)S(1)} %bitcast.78, f32[2,280,16,128]{3,2,1,0:T(8,128)} %param.21), kind=kOutput, calls=%fused_computation.34 | convolution fusion | flops 880803840 | bytes 22937600 | tf_op jit(solution)/shard_map/nij,njk->nik/dot_general | solution.py:206
  1106.5 10.2 all-gather.6.cloned.1.call-done
  1116.6 10.6 fusion.54
  1127.3 1.0 copy.31
  1128.2 0.6 copy-done.7
  1128.9 1.0 copy.32
  (105 shorter events, 3.1 us)
Async XLA Ops:
  7.2 8.2 copy-start.23
  7.2 226.6 %all-gather.4.cloned.1.call-start = ((), (), s32[]{:S(2)}) async-start(), calls=%async_computation.9 | async-start | bytes 45875200 | tf_op jit(solution)/shard_map/all_gather | solution.py:82
  7.9 37.7 %copy-start.22 = (bf16[2,256]{1,0:T(2,128)(2,1)S(1)}, bf16[2,256]{1,0:T(2,128)(2,1)}, u32[]{:S(2)}) copy-start(bf16[2,256]{1,0:T(2,128)(2,1)} %param.17) | copy-start | bytes 3076
  7.9 42.9 %copy-start.21 = (bf16[3,256]{1,0:T(4,128)(2,1)S(1)}, bf16[3,256]{1,0:T(4,128)(2,1)}, u32[]{:S(2)}) copy-start(bf16[3,256]{1,0:T(4,128)(2,1)} %param.18) | copy-start | bytes 4612
  7.9 48.2 %copy-start.24 = (s32[8]{0:T(128)S(1)}, s32[8]{0:T(128)}, u32[]{:S(2)}) copy-start(s32[8]{0:T(128)} %param.14) | copy-start | bytes 100
  7.9 33.2 %all-to-all-start = ((bf16[8,64,1024]{2,1,0:T(8,128)(2,1)}), bf16[8,64,1024]{2,1,0:T(8,128)(2,1)S(1)}, u32[]{:S(2)}, u32[]{:S(2)}) async-start(bf16[8,64,1024]{2,1,0:T(8,128)(2,1)} %bitcast), calls=%async_computation | async-start | bytes 2097152 | tf_op jit(solution)/shard_map/all_to_all | solution.py:72
  41.1 29.8 %all-to-all-start.2 = ((bf16[8,64,1024]{2,1,0:T(8,128)(2,1)}), bf16[8,64,1024]{2,1,0:T(8,128)(2,1)}, u32[]{:S(2)}, u32[]{:S(2)}) async-start(bf16[8,64,1024]{2,1,0:T(8,128)(2,1)} %bitcast.10), calls=%async_computation.2 | async-start | bytes 2097152 | tf_op jit(solution)/shard_map/all_to_all | solution.py:75
  45.4 325.4 %reduce-scatter.8.cloned.1.call-start = ((), (), s32[]{:S(2)}) async-start(), calls=%async_computation.11 | async-start | bytes 2621440 | tf_op jit(solution)/shard_map/reduce_scatter | solution.py:159
  74.1 159.7 %copy-start.18 = (bf16[512,1024]{1,0:T(8,128)(2,1)}, bf16[512,1024]{1,0:T(8,128)(2,1)S(1)}, u32[]{:S(2)}) copy-start(bf16[512,1024]{1,0:T(8,128)(2,1)S(1)} %fusion.32) | copy-start | bytes 3145732
  239.3 5.4 copy-start
  239.3 4.2 copy-start.5
  239.8 4.9 collective-permute-start
  247.0 3.3 copy-start.16
  250.3 18.3 %copy-start.10 = (f32[512,1024]{1,0:T(8,128)}, f32[512,1024]{1,0:T(8,128)S(1)}, u32[]{:S(2)}) copy-start(f32[512,1024]{1,0:T(8,128)S(1)} %get-tuple-element.51) | copy-start | bytes 6291460
  286.4 16.0 %copy-start.8 = (bf16[8,64,1024]{2,1,0:T(8,128)(2,1)S(1)}, bf16[8,64,1024]{2,1,0:T(8,128)(2,1)}, u32[]{:S(2)}) copy-start(bf16[8,64,1024]{2,1,0:T(8,128)(2,1)} %broadcast_select_fusion.2) | copy-start | bytes 3145732
  286.4 16.0 %copy-start.11 = (f32[512,1024]{1,0:T(8,128)S(1)}, f32[512,1024]{1,0:T(8,128)}, u32[]{:S(2)}) copy-start(f32[512,1024]{1,0:T(8,128)} %copy-done.10) | copy-start | bytes 6291460
  302.4 2.2 copy-start.17
  303.2 1.5 copy-start.2
  307.3 93.6 %reduce-scatter.6.cloned.1.call-start = ((), (), s32[]{:S(2)}) async-start(), calls=%async_computation.10 | async-start | bytes 7864320 | tf_op jit(solution)/shard_map/reduce_scatter | solution.py:156
  307.3 3.7 copy-start.1
  307.4 12.3 %slice-start = ((s8[6291456]{0:T(1024)(128)(4,1)}), s8[4194304]{0:T(1024)(128)(4,1)S(1)}, s32[]{:S(2)}) async-start(s8[6291456]{0:T(1024)(128)(4,1)} %bitcast.80), calls=%async_computation.17 | async-start | bytes 8388608
  311.0 8.6 slice-start.1
  313.4 9.4 copy-start.13
  313.5 5.8 collective-permute-start.1
  322.2 1.0 copy-start.14
  322.2 2.0 copy-start.19
  322.8 1.0 copy-start.15
  329.9 1.2 copy-start.9
  329.9 151.9 %reduce-scatter.12.cloned.1.call-start = ((), (), s32[]{:S(2)}) async-start(), calls=%async_computation.13 | async-start | bytes 11796480 | tf_op jit(solution)/shard_map/reduce_scatter | solution.py:165
  341.0 1.6 copy-start.12
  341.0 281.2 %reduce-scatter.10.cloned.1.call-start = ((), (), s32[]{:S(2)}) async-start(), calls=%async_computation.12 | async-start | bytes 23592960 | tf_op jit(solution)/shard_map/reduce_scatter | solution.py:162
  360.4 346.9 %reduce-scatter.14.cloned.1.call-start = ((), (), s32[]{:S(2)}) async-start(), calls=%async_computation.14 | async-start | bytes 20480 | tf_op jit(solution)/shard_map/reduce_scatter | solution.py:168
  370.7 610.2 %all-reduce.3.cloned.1.call-start = ((), (), s32[]{:S(2)}) async-start(), calls=%async_computation.16 | async-start | bytes 18350080 | tf_op jit(solution)/shard_map/psum | solution.py:176
  622.2 494.4 %all-gather.6.cloned.1.call-start = ((), (), s32[]{:S(2)}) async-start(), calls=%async_computation.15 | async-start | bytes 10321920 | tf_op jit(solution)/shard_map/all_gather | solution.py:203
  636.0 3.0 copy-start.3
  642.2 1.9 copy-start.4
  645.4 111.4 %copy-start.20 = (f32[5,256]{1,0:T(8,128)S(1)}, f32[5,256]{1,0:T(8,128)}, u32[]{:S(2)}) copy-start(f32[5,256]{1,0:T(8,128)} %param.19) | copy-start | bytes 15364
  703.6 54.7 %all-to-all-start.3 = ((bf16[8,64,1024]{2,1,0:T(8,128)(2,1)}), bf16[8,64,1024]{2,1,0:T(8,128)(2,1)S(1)}, u32[]{:S(2)}, u32[]{:S(2)}) async-start(bf16[8,64,1024]{2,1,0:T(8,128)(2,1)} %get-tuple-element.48), calls=%async_computation.3 | async-start | bytes 2097152 | tf_op jit(solution)/shard_map/all_to_all | solution.py:153
  758.3 222.7 %copy-start.6 = (bf16[8,64,1024]{2,1,0:T(8,128)(2,1)}, bf16[8,64,1024]{2,1,0:T(8,128)(2,1)S(1)}, u32[]{:S(2)}) copy-start(bf16[8,64,1024]{2,1,0:T(8,128)(2,1)S(1)} %all-to-all-done.3) | copy-start | bytes 3145732
  991.1 31.2 %slice-start.2 = ((s8[4587520]{0:T(1024)(128)(4,1)}), s8[393216]{0:T(1024)(128)(4,1)S(1)}, s32[]{:S(2)}) async-start(s8[4587520]{0:T(1024)(128)(4,1)} %bitcast.82), calls=%async_computation.19 | async-start | bytes 786432
  1010.3 12.0 %slice-start.3 = ((s8[4587520]{0:T(1024)(128)(4,1)}), s8[4194304]{0:T(1024)(128)(4,1)S(1)}, s32[]{:S(2)}) async-start(s8[4587520]{0:T(1024)(128)(4,1)} %bitcast.82), calls=%async_computation.20 | async-start | bytes 8388608
  1127.3 1.6 copy-start.7
Sparse Core Ops, SparseCore 0:
  9.6 224.1 all-gather.3
  307.4 31.9 reduce-scatter.7
  342.0 58.8 reduce-scatter.5
  403.9 77.9 reduce-scatter.11
  484.3 137.8 reduce-scatter.9
  625.0 19.4 reduce-scatter.13
  649.1 331.8 all-reduce.2
  983.0 133.6 all-gather.5
where the time goes:
time: 1140 us
  waiting for transfers between devices  689 us (60%)
  matrix products  212 us (19%)
  blocking collectives  118 us (10%)
  local copies, waits for them, and re-layouts  51.4 us (5%)
  other arithmetic  30.2 us (3%)
  starting transfers between devices  20.7 us (2%)
  between operations  14.9 us (1%)
    psum x1, waiting for transfers between devices, shards(): lax.psum(summed[3].astype(jnp.bfloat16), 'seq').astype(jnp.float32)  223 us
    all_gather x1, waiting for transfers between devices, shards(): lax.all_gather(weights, 'wsh', axis=0, tiled=True)  160 us
    reduce_scatter x1, waiting for transfers between devices, shards(): lax.psum_scatter(g_gu.astype(jnp.bfloat16), 'wsh', scatter_dimension=0, t...  140 us
    reduce_scatter x1, waiting for transfers between devices, shards(): lax.psum_scatter(g_down.astype(jnp.bfloat16), 'wsh', scatter_dimension=0,...  81 us
    all_to_all x1, blocking collectives, shards(): lax.all_to_all(leaving[0], 'seq', split_axis=0, concat_axis=0, tiled=True)  58.2 us
    psum x1, blocking collectives, shards(): lax.psum(summed[4].astype(jnp.bfloat16), 'seq').astype(jnp.float32)  49.4 us
    dot_general x4, matrix products, contract_cols(): lax.dot_general(left, right, (((1,), (1,)), ((), ())), preferred_element_...  39.1 us
    dot_general x4, matrix products, contract_rows(): lax.dot_general(left, right, (((0,), (0,)), ((), ())), preferred_element_...  36 us
  transfers between devices with their start and end apart: 13, of which 10 were waited for; matrix products, arithmetic and copies ran while one was open for 18% of the time, Pallas kernels for 0%

commit v1 on v0

--- a/solution.py
+++ b/solution.py
@@ -1,3 +1,4 @@
+import functools
 import jax
 import jax.numpy as jnp
 from jax import lax
@@ -12,6 +13,34 @@
 LEARN = 0.03
 LEARN_VEC = 0.05
 HIGH = lax.Precision.HIGHEST
+
+
+def play_the_lines(chunk, ndim_at):
+    chunk = jnp.moveaxis(chunk, 0, ndim_at)
+    f_now = chunk.shape
+    return chunk.reshape(
+        *f_now[:ndim_at], f_now[ndim_at] * f_now[ndim_at + 1], *f_now[ndim_at + 2 :]
+    )
+
+
+def produce_tails(matrix, net_axis):
+    f_next, m_next = (lax.axis_size(net_axis), lax.axis_index(net_axis))
+    newest, d_next = (matrix[None], 1)
+    while d_next < f_next:
+        z2 = lax.ppermute(newest, net_axis, tuple(((h, h ^ d_next) for h in range(f_next))))
+        everything = m_next & d_next == 0
+        newest = jnp.concatenate(
+            [jnp.where(everything, newest, z2), jnp.where(everything, z2, newest)]
+        )
+        d_next *= 2
+    return newest
+
+
+def _recover_task(load, z_in, in_dim):
+    return play_the_lines(produce_tails(load, z_in), in_dim)
+
+
+rest_the_tables = functools.partial(_recover_task, z_in="wsh", in_dim=0)
 
 
 def passed_along(block, axis, distance):
@@ -79,7 +108,7 @@
     x_bf = jnp.take(arrived[0], deal_order, axis=0).reshape(rows, D)
     dy_bf = jnp.take(arrived[1], deal_order, axis=0).reshape(rows, D)
     full_w, gains_bf, kernel_bf = (
-        lax.all_gather(weights, "wsh", axis=0, tiled=True),
+        rest_the_tables(weights),
         lax.all_gather(norm_gains, "wsh", axis=1, tiled=True),
         lax.all_gather(conv_kernel, "wsh", axis=1, tiled=True),
     )

time: 1140 us -> 1410 us (1.24)
  blocking collectives: 118 us -> 472 us
  waiting for transfers between devices: 689 us -> 533 us
  other arithmetic: 30.2 us -> 94.2 us
    all_gather x1, blocking collectives: 5.21 us -> 359 us  [shards(): lax.all_gather(norm_gains, 'wsh', axis=1, tiled=True)]
    all_gather x1 -> x0, waiting for transfers between devices: 160 us -> none  [shards(): lax.all_gather(weights, 'wsh', axis=0, tiled=True)]
    concatenate x0 -> x2, other arithmetic: none -> 35.4 us  [produce_tails(): jnp.concatenate([jnp.where(everything, newest, z2), jnp.where(everything,...]
    select_n x0 -> x2, other arithmetic: none -> 32 us  [produce_tails(): jnp.where(everything, newest, z2)]
    ppermute x0 -> x2, waiting for transfers between devices: none -> 14.3 us  [produce_tails(): lax.ppermute(newest, net_axis, tuple(((h, h ^ d_next) for h in range(f_ne...]
  transfers between devices with their start and end apart: 13 -> 14, of which waited for: 10 -> 10; matrix products, arithmetic and copies ran while one was open for 18% -> 15% of each run, Pallas kernels for 0% -> 0%
where the time goes in v1:
time: 1410 us; the launch traced here: 1400 us
  waiting for transfers between devices  533 us (38%)
  blocking collectives  472 us (33%)
  matrix products  211 us (15%)
  other arithmetic  94.2 us (7%)
  local copies, waits for them, and re-layouts  51.5 us (4%)
  starting transfers between devices  23.3 us (2%)
  between operations  15 us (1%)
    all_gather x1, blocking collectives, shards(): lax.all_gather(norm_gains, 'wsh', axis=1, tiled=True)  359 us
    psum x1, waiting for transfers between devices, shards(): lax.psum(summed[3].astype(jnp.bfloat16), 'seq').astype(jnp.float32)  223 us
    reduce_scatter x1, waiting for transfers between devices, shards(): lax.psum_scatter(g_gu.astype(jnp.bfloat16), 'wsh', scatter_dimension=0, t...  140 us
    reduce_scatter x1, waiting for transfers between devices, shards(): lax.psum_scatter(g_down.astype(jnp.bfloat16), 'wsh', scatter_dimension=0,...  81.1 us
    all_to_all x1, blocking collectives, shards(): lax.all_to_all(leaving[0], 'seq', split_axis=0, concat_axis=0, tiled=True)  58.3 us
    psum x1, blocking collectives, shards(): lax.psum(summed[4].astype(jnp.bfloat16), 'seq').astype(jnp.float32)  49.4 us
    dot_general x4, matrix products, contract_cols(): lax.dot_general(left, right, (((1,), (1,)), ((), ())), preferred_element_...  39.4 us
    dot_general x4, matrix products, contract_rows(): lax.dot_general(left, right, (((0,), (0,)), ((), ())), preferred_element_...  35.7 us
  transfers between devices with their start and end apart: 14, of which 10 were waited for; matrix products, arithmetic and copies ran while one was open for 15% of the time, Pallas kernels for 0%

profile of v1, /device:TPU:0, one launch (start us, length us, event | category | flops | bytes accessed | tf_op | source)
XLA Modules:
  0.0 1400.6 jit_solution(8099678602235878044)
XLA Ops:
  7.7 14.3 %collective-permute-done = bf16[1,256,17920]{2,1,0:T(8,128)(2,1)} collective-permute-done((bf16[1,256,17920]{2,1,0:T(8,128)(2,1)}, bf16[1,256,17920]{2,1,0:T(8,128)(2,1)}, u32[]{:S(2)}, u32[]{:S(2)}) %collective-permute-start) | collective-permute-done | bytes 9175072 | tf_op jit(solution)/shard_map/ppermute | solution.py:30
  22.0 7.3 broadcast_select_fusion.3
  29.3 11.2 pad_maximum_fusion.1
  40.5 0.7 copy-done.1
  41.2 2.9 collective-permute-start.1
  44.0 5.8 all-to-all-start
  50.0 25.6 %all-to-all-done = bf16[8,64,1024]{2,1,0:T(8,128)(2,1)S(1)} async-done(((bf16[8,64,1024]{2,1,0:T(8,128)(2,1)}), bf16[8,64,1024]{2,1,0:T(8,128)(2,1)S(1)}, u32[]{:S(2)}, u32[]{:S(2)}) %all-to-all-start) | async-done | bytes 1048608 | tf_op jit(solution)/shard_map/all_to_all | solution.py:101
  75.6 4.2 all-to-all-start.2
  80.1 359.3 %all_gather.9 = bf16[2,1024]{1,0:T(2,128)(2,1)S(1)} all-gather(bf16[2,256]{1,0:T(2,128)(2,1)S(1)} %copy-done.28), channel_id=1, replica_groups=mesh['seq'=8,'wsh'=4] {'wsh'}, dimensions={1}, use_global_device_ids=true | all-gather | bytes 5120 | tf_op jit(solution)/shard_map/all_gather | solution.py:112
  439.4 5.2 all_gather.10
  444.7 0.6 gather_fusion
  445.9 1.8 gather_fusion.2
  448.1 24.7 %broadcast_select_fusion.1 = (bf16[2,256,17920]{2,1,0:T(8,128)(2,1)}, bf16[2,256,17920]{2,1,0:T(8,128)(2,1)}) fusion(bf16[2,256,17920]{2,1,0:T(8,128)(2,1)} %collective-permute-done.1, pred[]{:T(512)S(6)} %eq.6, bf16[1,256,17920]{2,1,0:T(8,128)(2,1)} %copy-done.1, bf16[1,256,17920]{2,1,0:T(8,128)(2,1)} %copy-done), kind=kLoop, calls=%fused_computation.10 | loop fusion | flops 27525120 | bytes 73400320 | tf_op jit(solution)/shard_map/jit(_where)/select_n | solution.py:33
  472.8 24.2 %pad_maximum_fusion = bf16[4,256,17920]{2,1,0:T(8,128)(2,1)} fusion(bf16[2,256,17920]{2,1,0:T(8,128)(2,1)} %get-tuple-element.32, bf16[2,256,17920]{2,1,0:T(8,128)(2,1)} %get-tuple-element.31), kind=kLoop, calls=%fused_computation.4 | loop fusion | flops 18350080 | bytes 73400320 | tf_op jit(solution)/shard_map/concatenate | solution.py:32
  497.0 5.5 fusion.14
  503.0 4.0 collective-permute-start.2
  507.2 0.7 collective-permute-done.2
  507.9 2.3 multiply_convert_fusion.7
  510.3 3.3 multiply_reduce_fusion.3
  513.6 18.2 %fusion.4 = f32[512,9216]{1,0:T(8,128)} fusion(bf16[1024,17920]{1,0:T(8,128)(2,1)} %bitcast.86, f32[512,1024]{1,0:T(8,128)S(1)} %get-tuple-element.55, f32[1024]{0:T(1024)S(1)} %bitcast.112, f32[512]{0:T(512)S(1)} %add_rsqrt_fusion.1), kind=kOutput, calls=%fused_computation.14 | convolution fusion | flops 9665249280 | bytes 39852032 | tf_op jit(solution)/shard_map/dot_general | solution.py:139
  531.8 16.9 %multiply_convert_fusion.1 = (bf16[512,4608]{1,0:T(8,128)(2,1)}, bf16[512,4608]{1,0:T(8,128)(2,1)}, bf16[512,4608]{1,0:T(8,128)(2,1)}) fusion(f32[512,9216]{1,0:T(8,128)} %fusion.4, bf16[512,1024]{1,0:T(8,128)(2,1)S(1)} %bitcast.99, bf16[1024,17920]{1,0:T(8,128)(2,1)} %bitcast.87), kind=kOutput, calls=%fused_computation.19 | convolution fusion | flops 4869586944 | bytes 43515904 | tf_op jit(solution)/shard_map/dot_general | solution.py:147
  548.8 15.9 %multiply_reduce_fusion.1 = (bf16[1024]{0:T(1024)(128)(2,1)S(1)}, f32[512]{0:T(512)S(1)}, f32[512,1024]{1,0:T(8,128)S(1)}) fusion(f32[512,1024]{1,0:T(8,128)} %copy-done.12, f32[512]{0:T(512)S(1)} %add_rsqrt_fusion.1, f32[1024]{0:T(1024)S(1)} %bitcast.113, bf16[1024,17920]{1,0:T(8,128)(2,1)} %bitcast.88, bf16[512,4608]{1,0:T(8,128)(2,1)} %get-tuple-element.34, ...), kind=kOutput, calls=%fused_computation.81 | convolution fusion | flops 9685694464 | bytes 32516096 | tf_op jit(solution)/shard_map/dot_general | solution.py:79
  564.7 0.7 subtract_add_fusion
  565.5 1.5 copy-done.5
  567.0 2.6 convolution_convert_fusion.3
  569.7 4.9 multiply_convert_fusion.4
  574.7 1.6 collective-permute-start.3
  576.2 4.5 collective-permute-done.3
  581.1 2.6 fusion.26
  585.7 5.8 convolution_convert_fusion.2
  591.6 1.1 copy-done.11
  592.8 9.8 convolution_convert_fusion.1
  602.7 1.5 copy-done.14
  604.2 17.4 %convolution_convert_fusion = bf16[1024,9216]{1,0:T(8,128)(2,1)} fusion(bf16[512,4608]{1,0:T(8,128)(2,1)} %get-tuple-element.34, bf16[512,4608]{1,0:T(8,128)(2,1)} %get-tuple-element.33, f32[512,1024]{1,0:T(8,128)S(1)} %copy-done.14, f32[1024]{0:T(1024)S(1)} %bitcast.115, f32[512]{0:T(512)S(1)} %add_rsqrt_fusion.1), kind=kOutput, calls=%fused_computation.11 | convolution fusion | flops 9693560832 | bytes 30414848 | tf_op jit(solution)/shard_map/dot_general | solution.py:73
  622.3 8.8 fusion.41
  631.1 0.6 concatenate.38
  631.8 32.6 %reduce-scatter.6.cloned.1.call-done = bf16[256,3072]{1,0:T(8,128)(2,1)} async-done(((bf16[1024,3072]{1,0:T(8,128)(2,1)}), bf16[256,3072]{1,0:T(8,128)(2,1)}) %reduce-scatter.6.cloned.1.call-update) | async-done | bytes 1572880 | tf_op jit(solution)/shard_map/reduce_scatter | solution.py:185
  664.4 81.1 %reduce-scatter.12.cloned.1.call-done = bf16[256,4608]{1,0:T(8,128)(2,1)} async-done(((bf16[1024,4608]{1,0:T(8,128)(2,1)}), bf16[256,4608]{1,0:T(8,128)(2,1)}) %reduce-scatter.12.cloned.1.call-update) | async-done | bytes 2359312 | tf_op jit(solution)/shard_map/reduce_scatter | solution.py:194
  745.6 140.3 %reduce-scatter.10.cloned.1.call-done = bf16[256,9216]{1,0:T(8,128)(2,1)} async-done(((bf16[1024,9216]{1,0:T(8,128)(2,1)}), bf16[256,9216]{1,0:T(8,128)(2,1)}) %reduce-scatter.10.cloned.1.call-update) | async-done | bytes 4718608 | tf_op jit(solution)/shard_map/reduce_scatter | solution.py:191
  886.0 2.8 slice.250
  888.8 1.0 sort.17
  889.8 9.9 add_convert_fusion
  899.7 3.0 gather_fusion.1
  902.6 3.3 fusion.37
  905.9 1.9 gather_fusion.3
  907.8 1.2 broadcast_select_fusion.4
  909.1 58.3 %all_to_all.20 = bf16[8,64,1024]{2,1,0:T(8,128)(2,1)S(1)} all-to-all(bf16[8,64,1024]{2,1,0:T(8,128)(2,1)S(1)} %get-tuple-element.53), channel_id=1, replica_groups=mesh['seq'=8,'wsh'=4] {'seq'}, dimensions={0} | all-to-all | bytes 2097152 | tf_op jit(solution)/shard_map/all_to_all | solution.py:181
  967.4 3.7 all-to-all-start.3
  971.1 49.4 %psum.39 = bf16[5,256]{1,0:T(8,128)(2,1)S(1)} all-reduce(bf16[5,256]{1,0:T(8,128)(2,1)} %reduce-scatter.14.cloned.1.call-done), channel_id=1, replica_groups=mesh['seq'=8,'wsh'=4] {'seq'}, use_global_device_ids=true, to_apply=%region_21.23 | all-reduce | flops 1280 | bytes 5120 | tf_op jit(solution)/shard_map/psum | solution.py:206
  1020.5 0.6 fusion.63
  1021.1 0.9 all-to-all-done.3
  1022.0 222.6 %all-reduce.3.cloned.1.call-done = (bf16[256,4608]{1,0:T(8,128)(2,1)}, bf16[256,9216]{1,0:T(8,128)(2,1)}, bf16[256,1024]{1,0:T(8,128)(2,1)}, bf16[256,3072]{1,0:T(8,128)(2,1)}) async-done(((bf16[256,4608]{1,0:T(8,128)(2,1)}, bf16[256,9216]{1,0:T(8,128)(2,1)}, bf16[256,1024]{1,0:T(8,128)(2,1)}, bf16[256,3072]{1,0:T(8,128)(2,1)}), (bf16[256,4608]{1,0:T(8,128)(2,1)}, bf16[256,9216]{1,0:T(8,128)(2,1)}, ...) | async-done | bytes 9175056 | tf_op jit(solution)/shard_map/psum | solution.py:205
  1244.6 10.2 convert_multiply_fusion
  1254.8 19.2 %mul.433 = f32[2,128,140,128]{3,2,1,0:T(8,128)} reshape(f32[256,17920]{1,0:T(8,128)} %convert_multiply_fusion) | data formatting | bytes 36700160 | tf_op jit(solution)/shard_map/mul | solution.py:209
  1274.0 12.0 copy.22
  1286.0 29.5 %fusion.19 = f32[1,280,16,128]{3,2,1,0:T(8,128)S(1)} fusion(f32[2,280,16,128]{3,2,1,0:T(8,128)S(1)} %bitcast.95, f32[280,128,128]{2,1,0:T(8,128)S(1)} %bitcast.80, s32[]{:T(128)S(6)} %select_n.46), kind=kOutput, calls=%fused_computation.45 | convolution fusion | flops 882524160 | bytes 25231364 | tf_op jit(solution)/shard_map/nij,nkj->nik/dot_general | solution.py:224
  1315.5 35.2 %fusion.18 = f32[1,280,16,128]{3,2,1,0:T(8,128)S(1)} fusion(f32[2,280,16,128]{3,2,1,0:T(8,128)S(1)} %bitcast.95, f32[280,128,128]{2,1,0:T(8,128)S(1)} %bitcast.81, s32[]{:T(128)S(6)} %select_n.46), kind=kOutput, calls=%fused_computation.43 | convolution fusion | flops 882524160 | bytes 41287684 | tf_op jit(solution)/shard_map/nji,njk->nik/dot_general | solution.py:225
  1350.8 2.4 pad_maximum_fusion.5
  1353.2 17.0 %fusion.16 = f32[280,128,16]{1,2,0:T(8,128)S(1)} fusion(f32[280,128,128]{2,1,0:T(8,128)S(1)} %bitcast.82, f32[2,280,16,128]{3,2,1,0:T(8,128)} %param.21), kind=kOutput, calls=%fused_computation.40 | convolution fusion | flops 880803840 | bytes 22937600 | tf_op jit(solution)/shard_map/nij,njk->nik/dot_general | solution.py:235
  1370.2 10.2 all-gather.3.cloned.1.call-done
  1380.4 10.6 fusion.54
  1391.0 1.0 copy.31
  1392.0 0.6 copy-done.9
  1392.6 1.0 copy.32
  (123 shorter events, 5.9 us)
Async XLA Ops:
  7.2 14.8 %collective-permute-start = (bf16[1,256,17920]{2,1,0:T(8,128)(2,1)}, bf16[1,256,17920]{2,1,0:T(8,128)(2,1)}, u32[]{:S(2)}, u32[]{:S(2)}) collective-permute-start(bf16[1,256,17920]{2,1,0:T(8,128)(2,1)} %bitcast.96), channel_id=1, source_target_pairs={{0,1},{1,0},{2,3},{3,2},{4,5},{5,4},{6,7},{7,6},{8,9},{9,8},{10,11... | collective-permute-start | bytes 27525128 | tf_op jit(solution)/shard_map/ppermute | solution.py:30
  29.3 11.2 copy-start
  29.3 11.9 copy-start.1
  29.3 20.6 %copy-start.29 = (s32[1,4]{1,0:T(1,128)S(1)}, s32[1,4]{1,0:T(1,128)}, u32[]{:S(2)}) copy-start(s32[1,4]{1,0:T(1,128)} %param.15) | copy-start | bytes 52
  41.2 38.9 %copy-start.28 = (bf16[2,256]{1,0:T(2,128)(2,1)S(1)}, bf16[2,256]{1,0:T(2,128)(2,1)}, u32[]{:S(2)}) copy-start(bf16[2,256]{1,0:T(2,128)(2,1)} %param.17) | copy-start | bytes 3076
  41.2 398.3 %copy-start.27 = (bf16[3,256]{1,0:T(4,128)(2,1)S(1)}, bf16[3,256]{1,0:T(4,128)(2,1)}, u32[]{:S(2)}) copy-start(bf16[3,256]{1,0:T(4,128)(2,1)} %param.18) | copy-start | bytes 4612
  41.2 403.5 %copy-start.30 = (s32[8]{0:T(128)S(1)}, s32[8]{0:T(128)}, u32[]{:S(2)}) copy-start(s32[8]{0:T(128)} %param.14) | copy-start | bytes 100
  41.2 406.9 %collective-permute-start.1 = (bf16[2,256,17920]{2,1,0:T(8,128)(2,1)}, bf16[2,256,17920]{2,1,0:T(8,128)(2,1)}, u32[]{:S(2)}, u32[]{:S(2)}) collective-permute-start(bf16[2,256,17920]{2,1,0:T(8,128)(2,1)} %pad_maximum_fusion.1), channel_id=1, source_target_pairs={{0,2},{1,3},{2,0},{3,1},{4,6},{5,7},{6,4},{7,5},{8,10},{9,11},{10,... | collective-permute-start | bytes 55050248 | tf_op jit(solution)/shard_map/ppermute | solution.py:30
  44.0 31.6 %all-to-all-start = ((bf16[8,64,1024]{2,1,0:T(8,128)(2,1)}), bf16[8,64,1024]{2,1,0:T(8,128)(2,1)S(1)}, u32[]{:S(2)}, u32[]{:S(2)}) async-start(bf16[8,64,1024]{2,1,0:T(8,128)(2,1)} %bitcast), calls=%async_computation | async-start | bytes 2097152 | tf_op jit(solution)/shard_map/all_to_all | solution.py:101
  75.6 370.2 %all-to-all-start.2 = ((bf16[8,64,1024]{2,1,0:T(8,128)(2,1)}), bf16[8,64,1024]{2,1,0:T(8,128)(2,1)}, u32[]{:S(2)}, u32[]{:S(2)}) async-start(bf16[8,64,1024]{2,1,0:T(8,128)(2,1)} %bitcast.12), calls=%async_computation.2 | async-start | bytes 2097152 | tf_op jit(solution)/shard_map/all_to_all | solution.py:104
  79.9 551.9 %reduce-scatter.8.cloned.1.call-start = ((), (), s32[]{:S(2)}) async-start(), calls=%async_computation.10 | async-start | bytes 2621440 | tf_op jit(solution)/shard_map/reduce_scatter | solution.py:188
  444.7 3.0 copy-start.22
  445.9 26.9 %copy-start.24 = (f32[512]{0:T(512)}, f32[512]{0:T(512)S(1)}, u32[]{:S(2)}) copy-start(f32[512]{0:T(512)S(1)} %rsqrt.23) | copy-start | bytes 6148
  448.1 49.0 %copy-start.19 = (bf16[512,1024]{1,0:T(8,128)(2,1)}, bf16[512,1024]{1,0:T(8,128)(2,1)S(1)}, u32[]{:S(2)}) copy-start(bf16[512,1024]{1,0:T(8,128)(2,1)S(1)} %fusion.32) | copy-start | bytes 3145732
  502.5 5.4 copy-start.2
  503.0 7.3 copy-start.3
  503.0 4.9 collective-permute-start.2
  507.2 57.5 %copy-start.10 = (bf16[8,64,1024]{2,1,0:T(8,128)(2,1)}, bf16[8,64,1024]{2,1,0:T(8,128)(2,1)S(1)}, u32[]{:S(2)}) copy-start(bf16[8,64,1024]{2,1,0:T(8,128)(2,1)S(1)} %broadcast_select_fusion.6) | copy-start | bytes 3145732
  510.3 3.3 copy-start.17
  513.6 18.2 %copy-start.12 = (f32[512,1024]{1,0:T(8,128)}, f32[512,1024]{1,0:T(8,128)S(1)}, u32[]{:S(2)}) copy-start(f32[512,1024]{1,0:T(8,128)S(1)} %get-tuple-element.55) | copy-start | bytes 6291460
  548.8 15.9 %copy-start.13 = (f32[512,1024]{1,0:T(8,128)S(1)}, f32[512,1024]{1,0:T(8,128)}, u32[]{:S(2)}) copy-start(f32[512,1024]{1,0:T(8,128)} %copy-done.12) | copy-start | bytes 6291460
  564.7 2.3 copy-start.18
  565.5 1.5 copy-start.5
  567.0 14.1 %slice-start = ((s8[6291456]{0:T(1024)(128)(4,1)}), s8[2097152]{0:T(1024)(128)(4,1)S(1)}, s32[]{:S(2)}) async-start(s8[6291456]{0:T(1024)(128)(4,1)} %bitcast.92), calls=%async_computation.16 | async-start | bytes 4194304
  569.6 94.8 %reduce-scatter.6.cloned.1.call-start = ((), (), s32[]{:S(2)}) async-start(), calls=%async_computation.9 | async-start | bytes 7864320 | tf_op jit(solution)/shard_map/reduce_scatter | solution.py:185
  569.7 11.4 slice-start.1
  574.6 9.6 copy-start.21
  574.6 6.5 copy-start.4
  574.7 6.1 collective-permute-start.3
  583.7 1.0 copy-start.15
  583.7 2.0 copy-start.20
  584.2 1.0 copy-start.16
  591.5 1.2 copy-start.11
  591.6 154.0 %reduce-scatter.12.cloned.1.call-start = ((), (), s32[]{:S(2)}) async-start(), calls=%async_computation.12 | async-start | bytes 11796480 | tf_op jit(solution)/shard_map/reduce_scatter | solution.py:194
  602.6 1.6 copy-start.14
  602.6 283.3 %reduce-scatter.10.cloned.1.call-start = ((), (), s32[]{:S(2)}) async-start(), calls=%async_computation.11 | async-start | bytes 23592960 | tf_op jit(solution)/shard_map/reduce_scatter | solution.py:191
  621.6 0.7 copy-start.23
  621.6 0.7 copy-start.25
  621.6 349.5 %reduce-scatter.14.cloned.1.call-start = ((), (), s32[]{:S(2)}) async-start(), calls=%async_computation.13 | async-start | bytes 20480 | tf_op jit(solution)/shard_map/reduce_scatter | solution.py:197
  631.7 612.9 %all-reduce.3.cloned.1.call-start = ((), (), s32[]{:S(2)}) async-start(), calls=%async_computation.15 | async-start | bytes 18350080 | tf_op jit(solution)/shard_map/psum | solution.py:205
  885.9 2.9 copy-start.31
  885.9 494.4 %all-gather.3.cloned.1.call-start = ((), (), s32[]{:S(2)}) async-start(), calls=%async_computation.14 | async-start | bytes 10321920 | tf_op jit(solution)/shard_map/all_gather | solution.py:232
  899.7 3.0 copy-start.6
  905.9 1.9 copy-start.7
  909.1 111.4 %copy-start.26 = (f32[5,256]{1,0:T(8,128)S(1)}, f32[5,256]{1,0:T(8,128)}, u32[]{:S(2)}) copy-start(f32[5,256]{1,0:T(8,128)} %param.19) | copy-start | bytes 15364
  967.4 54.7 %all-to-all-start.3 = ((bf16[8,64,1024]{2,1,0:T(8,128)(2,1)}), bf16[8,64,1024]{2,1,0:T(8,128)(2,1)S(1)}, u32[]{:S(2)}, u32[]{:S(2)}) async-start(bf16[8,64,1024]{2,1,0:T(8,128)(2,1)} %get-tuple-element.52), calls=%async_computation.3 | async-start | bytes 2097152 | tf_op jit(solution)/shard_map/all_to_all | solution.py:182
  1022.0 222.6 %copy-start.8 = (bf16[8,64,1024]{2,1,0:T(8,128)(2,1)}, bf16[8,64,1024]{2,1,0:T(8,128)(2,1)S(1)}, u32[]{:S(2)}) copy-start(bf16[8,64,1024]{2,1,0:T(8,128)(2,1)S(1)} %all-to-all-done.3) | copy-start | bytes 3145732
  1254.8 31.2 %slice-start.2 = ((s8[4587520]{0:T(1024)(128)(4,1)}), s8[393216]{0:T(1024)(128)(4,1)S(1)}, s32[]{:S(2)}) async-start(s8[4587520]{0:T(1024)(128)(4,1)} %bitcast.94), calls=%async_computation.18 | async-start | bytes 786432
  1274.0 12.0 slice-start.3
  1391.0 1.6 copy-start.9
Sparse Core Ops, SparseCore 0:
  569.8 33.2 reduce-scatter.7
  605.6 58.8 reduce-scatter.5
  667.6 77.8 reduce-scatter.11
  748.0 137.8 reduce-scatter.9
  888.7 19.5 reduce-scatter.13
  912.7 331.8 all-reduce.2
  1246.7 133.6 all-gather.2
